TPU v7x, 32 devices: a whole 2x2x4 slice. The times are simulated.
32 devices in a mesh: usr: 8 (over y, x, core), itm: 4 (over z).
Axes of the slice: x: 2, y: 2, z: 4, core: 2. Of those that a mesh axis runs over, the one named last changes fastest.
Arguments:
- ratings: bfloat16 [8192, 8192], P('usr', 'itm'), may hold values from -6 to 6
- tile_mask: int32 [64, 64], P('usr', 'itm'), may hold values 0 or 1
- counts: int32 [8], P('usr'), may hold values from 256 to 1024
- users: float32 [8192, 256], P(('usr', 'itm')), may hold values from -1.5 to 1.5
- items: float32 [8192, 256], P(('itm', 'usr')), may hold values from -1.5 to 1.5
- user_mom: float32 [8192, 256], P(('usr', 'itm')), may hold values from -6 to 6
- item_mom: float32 [8192, 256], P(('itm', 'usr')), may hold values from -6 to 6
- user_accept: int32 [64], P(('usr', 'itm')), may hold values 0 or 1
- item_accept: int32 [64], P(('itm', 'usr')), may hold values 0 or 1
Outputs:
- users_out: float32 [8192, 256], P(('usr', 'itm'))
- items_out: float32 [8192, 256], P(('itm', 'usr'))
- user_mom_out: float32 [8192, 256], P(('usr', 'itm'))
- item_mom_out: float32 [8192, 256], P(('itm', 'usr'))
All inputs are finite; a program needn't handle non-finite values. No bound on the sum of `tile_mask` or of `user_accept` or of `item_accept` on one device may be relied on, other than what follows from the above.
Results may differ from a plain program's by a relative error of at most 0.01.
Values may be sent and summed in bfloat16 or wider, within the bound.
A program may use at most 64 MiB of HBM per device.

v0:
```python
import jax
import jax.numpy as jnp
from jax import lax
from jax.sharding import PartitionSpec as P

BLK = 128
LEAPS = 2


step_size = 0.02


def body(ratings, tile_mask, counts, users, items, user_mom, item_mom, user_accept, item_accept):
    group_rows = ratings.shape[0]
    colmask = jnp.repeat(tile_mask, BLK, axis=1).astype(jnp.float32)
    alive = (jnp.arange(group_rows, dtype=jnp.int32) < counts[0]).astype(jnp.float32)

    def gradients(user_pos, item_pos):
        full_users = lax.all_gather(user_pos.astype(jnp.bfloat16), "itm", axis=0, tiled=True)
        piece = lax.all_gather(item_pos.astype(jnp.bfloat16), "usr", axis=0, tiled=True)
        count = piece.shape[0]
        guess = jnp.dot(full_users, piece.T, preferred_element_type=jnp.float32)
        error = (ratings.astype(jnp.float32) - guess).reshape(
            group_rows // BLK, BLK, count
        ) * colmask[:, None, :]
        error = (error.reshape(group_rows, count) * alive[:, None]).astype(jnp.bfloat16)
        user_sum = jnp.dot(error, piece, preferred_element_type=jnp.float32)
        item_part = jnp.dot(error.T, full_users, preferred_element_type=jnp.float32)
        item_sum = item_part
        user_sum, item_sum = (user_sum, item_sum)
        user_part = lax.psum_scatter(
            user_sum.astype(jnp.bfloat16), "itm", scatter_dimension=0, tiled=True
        ).astype(jnp.float32)
        item_part = lax.psum_scatter(
            item_sum.astype(jnp.bfloat16), "usr", scatter_dimension=0, tiled=True
        ).astype(jnp.float32)
        return (user_pos - user_part, item_pos - item_part)

    user_pos, item_pos = (users, items)
    user_grad, item_grad = gradients(user_pos, item_pos)
    for leap in range(LEAPS):
        user_mom = user_mom - 0.5 * step_size * user_grad
        item_mom = item_mom - 0.5 * step_size * item_grad
        user_pos = user_pos + step_size * user_mom
        item_pos = item_pos + step_size * item_mom
        user_grad, item_grad = gradients(user_pos, item_pos)
        user_mom = user_mom - 0.5 * step_size * user_grad
        item_mom = item_mom - 0.5 * step_size * item_grad
    user_take = jnp.repeat(user_accept, BLK)[:, None] > 0
    item_take = jnp.repeat(item_accept, BLK)[:, None] > 0
    return (
        jnp.where(user_take, user_pos, users),
        jnp.where(item_take, item_pos, items),
        user_mom,
        item_mom,
    )


def solution(mesh):
    in_specs = (
        P("usr", "itm"),
        P("usr", "itm"),
        P("usr"),
        P(("usr", "itm"), None),
        P(("itm", "usr"), None),
        P(("usr", "itm"), None),
        P(("itm", "usr"), None),
        P(("usr", "itm")),
        P(("itm", "usr")),
    )
    out_specs = (
        P(("usr", "itm"), None),
        P(("itm", "usr"), None),
        P(("usr", "itm"), None),
        P(("itm", "usr"), None),
    )
    return jax.shard_map(body, mesh=mesh, in_specs=in_specs, out_specs=out_specs, check_vma=False)
```

profile of v0, /device:TPU:0, one launch (start us, length us, event | category | flops | bytes accessed | tf_op | source)
XLA Modules:
  0.0 297.7 jit_solution(13225695917955552715)
XLA Ops:
  7.2 0.0 all-gather.4.cloned.1.call-start
  7.2 1.6 convert_element_type.88
  8.8 0.0 all-gather.4.cloned.1.call-update
  8.9 0.0 reduce-scatter.9.cloned.1.call-start
  8.9 1.0 convert_element_type.87
  10.5 0.7 convert_element_type.89
  11.2 0.1 copy.13
  11.3 17.4 %all_gather.18 = bf16[1024,256]{1,0:T(8,128)(2,1)S(1)} all-gather(bf16[256,256]{1,0:T(8,128)(2,1)S(1)} %convert_element_type.87), channel_id=1, replica_groups=mesh['usr'=8,'itm'=4] {'itm'}, dimensions={0}, use_global_device_ids=true | all-gather | bytes 655360 | tf_op jit(solution)/shard_map/all_gather | solution.py:19
  28.7 0.1 broadcast_bitcast_fusion
  28.7 7.8 %all-gather.4.cloned.1.call-done = bf16[2048,256]{1,0:T(8,128)(2,1)} async-done(((bf16[256,256]{1,0:T(8,128)(2,1)}), bf16[2048,256]{1,0:T(8,128)(2,1)}) %all-gather.4.cloned.1.call-update) | async-done | bytes 1048592 | tf_op jit(solution)/shard_map/all_gather | solution.py:20
  36.6 4.0 %fusion.1 = bf16[1024,2048]{1,0:T(8,128)(2,1)S(1)} fusion(bf16[1024,2048]{1,0:T(8,128)(2,1)} %param.9, bf16[1024,256]{1,0:T(8,128)(2,1)S(1)} %all_gather.18, bf16[2048,256]{1,0:T(8,128)(2,1)} %all-gather.4.cloned.1.call-done, f32[1024]{0:T(1024)S(1)} %fusion.8, f32[8,2048]{1,0:T(8,128)S(1)} %broadcast_bitcast_fusion), kind=kOutput, calls=%fused_computation.7 | convolution fusion | flops 1084227584 | bytes 10031104 | tf_op jit(solution)/shard_map/dot_general | solution.py:22
  40.5 1.9 copy-done.3
  42.5 2.4 convolution_convert_fusion.2
  44.9 0.0 reduce-scatter.9.cloned.1.call-update
  45.0 0.0 reduce-scatter.7.cloned.1.call-start
  45.0 4.3 %convolution_convert_fusion.5 = bf16[1024,256]{1,0:T(8,128)(2,1)} fusion(bf16[1024,2048]{1,0:T(8,128)(2,1)} %copy-done.3, bf16[2048,256]{1,0:T(8,128)(2,1)S(1)} %copy-done.9), kind=kOutput, calls=%fused_computation.17 | convolution fusion | flops 1074003968 | bytes 5767168 | tf_op jit(solution)/shard_map/dot_general | solution.py:27
  49.4 0.0 all-gather.6.cloned.1.call-start
  49.4 31.6 %reduce-scatter.9.cloned.1.call-done = bf16[256,256]{1,0:T(8,128)(2,1)} async-done(((bf16[2048,256]{1,0:T(8,128)(2,1)}), bf16[256,256]{1,0:T(8,128)(2,1)}) %reduce-scatter.9.cloned.1.call-update) | async-done | bytes 131088 | tf_op jit(solution)/shard_map/reduce_scatter | solution.py:34
  81.0 1.6 fusion.10
  82.7 0.0 reduce-scatter.13.cloned.1.call-start
  82.7 22.4 %reduce-scatter.7.cloned.1.call-done = bf16[256,256]{1,0:T(8,128)(2,1)} async-done(((bf16[1024,256]{1,0:T(8,128)(2,1)}), bf16[256,256]{1,0:T(8,128)(2,1)}) %reduce-scatter.7.cloned.1.call-update) | async-done | bytes 131088 | tf_op jit(solution)/shard_map/reduce_scatter | solution.py:31
  105.2 1.0 fusion.9
  106.1 15.5 %all_gather.20 = bf16[1024,256]{1,0:T(8,128)(2,1)S(1)} all-gather(bf16[256,256]{1,0:T(8,128)(2,1)S(1)} %fusion.9), channel_id=1, replica_groups=mesh['usr'=8,'itm'=4] {'itm'}, dimensions={0}, use_global_device_ids=true | all-gather | bytes 655360 | tf_op jit(solution)/shard_map/all_gather | solution.py:19
  121.6 7.5 %all-gather.6.cloned.1.call-done = bf16[2048,256]{1,0:T(8,128)(2,1)} async-done(((bf16[256,256]{1,0:T(8,128)(2,1)}), bf16[2048,256]{1,0:T(8,128)(2,1)}) %all-gather.6.cloned.1.call-update) | async-done | bytes 1048592 | tf_op jit(solution)/shard_map/all_gather | solution.py:20
  129.1 4.0 %fusion.3 = bf16[1024,2048]{1,0:T(8,128)(2,1)S(1)} fusion(bf16[1024,2048]{1,0:T(8,128)(2,1)} %param.9, bf16[1024,256]{1,0:T(8,128)(2,1)S(1)} %all_gather.20, bf16[2048,256]{1,0:T(8,128)(2,1)} %all-gather.6.cloned.1.call-done, f32[1024]{0:T(1024)S(1)} %fusion.8, f32[8,2048]{1,0:T(8,128)S(1)} %broadcast_bitcast_fusion), kind=kOutput, calls=%fused_computation.9 | convolution fusion | flops 1084227584 | bytes 10031104 | tf_op jit(solution)/shard_map/dot_general | solution.py:22
  133.1 1.9 copy-done.4
  135.0 2.4 convolution_convert_fusion.1
  137.5 0.0 reduce-scatter.11.cloned.1.call-start
  137.5 4.3 %convolution_convert_fusion.4 = bf16[1024,256]{1,0:T(8,128)(2,1)} fusion(bf16[1024,2048]{1,0:T(8,128)(2,1)} %copy-done.4, bf16[2048,256]{1,0:T(8,128)(2,1)S(1)} %copy-done.10), kind=kOutput, calls=%fused_computation.16 | convolution fusion | flops 1074003968 | bytes 5767168 | tf_op jit(solution)/shard_map/dot_general | solution.py:27
  141.9 0.0 all-gather.8.cloned.1.call-start
  141.9 31.7 %reduce-scatter.13.cloned.1.call-done = bf16[256,256]{1,0:T(8,128)(2,1)} async-done(((bf16[2048,256]{1,0:T(8,128)(2,1)}), bf16[256,256]{1,0:T(8,128)(2,1)}) %reduce-scatter.13.cloned.1.call-update) | async-done | bytes 131088 | tf_op jit(solution)/shard_map/reduce_scatter | solution.py:34
  173.6 1.7 fusion.7
  175.3 0.0 reduce-scatter.15.cloned.1.call-start
  175.4 22.2 %reduce-scatter.11.cloned.1.call-done = bf16[256,256]{1,0:T(8,128)(2,1)} async-done(((bf16[1024,256]{1,0:T(8,128)(2,1)}), bf16[256,256]{1,0:T(8,128)(2,1)}) %reduce-scatter.11.cloned.1.call-update) | async-done | bytes 131088 | tf_op jit(solution)/shard_map/reduce_scatter | solution.py:31
  197.6 1.0 fusion.6
  198.6 15.5 %all_gather.22 = bf16[1024,256]{1,0:T(8,128)(2,1)S(1)} all-gather(bf16[256,256]{1,0:T(8,128)(2,1)S(1)} %fusion.6), channel_id=1, replica_groups=mesh['usr'=8,'itm'=4] {'itm'}, dimensions={0}, use_global_device_ids=true | all-gather | bytes 655360 | tf_op jit(solution)/shard_map/all_gather | solution.py:19
  214.1 7.7 %all-gather.8.cloned.1.call-done = bf16[2048,256]{1,0:T(8,128)(2,1)} async-done(((bf16[256,256]{1,0:T(8,128)(2,1)}), bf16[2048,256]{1,0:T(8,128)(2,1)}) %all-gather.8.cloned.1.call-update) | async-done | bytes 1048592 | tf_op jit(solution)/shard_map/all_gather | solution.py:20
  221.7 4.0 %fusion.5 = bf16[1024,2048]{1,0:T(8,128)(2,1)S(1)} fusion(bf16[1024,2048]{1,0:T(8,128)(2,1)} %param.9, bf16[1024,256]{1,0:T(8,128)(2,1)S(1)} %all_gather.22, bf16[2048,256]{1,0:T(8,128)(2,1)} %all-gather.8.cloned.1.call-done, f32[1024]{0:T(1024)S(1)} %fusion.8, f32[8,2048]{1,0:T(8,128)S(1)} %broadcast_bitcast_fusion), kind=kOutput, calls=%fused_computation.11 | convolution fusion | flops 1084227584 | bytes 10031104 | tf_op jit(solution)/shard_map/dot_general | solution.py:22
  225.8 1.9 copy-done.2
  227.8 2.1 convolution_convert_fusion.3
  229.9 0.0 reduce-scatter.17.cloned.1.call-start
  229.9 4.6 %convolution_convert_fusion = bf16[2048,256]{1,0:T(8,128)(2,1)} fusion(bf16[1024,2048]{1,0:T(8,128)(2,1)} %copy-done.2, bf16[1024,256]{1,0:T(8,128)(2,1)S(1)} %all_gather.22), kind=kOutput, calls=%fused_computation.12 | convolution fusion | flops 1074266112 | bytes 5767168 | tf_op jit(solution)/shard_map/dot_general | solution.py:28
  234.6 0.1 broadcast_bitcast_fusion.2
  234.6 0.1 broadcast_bitcast_fusion.1
  234.7 17.1 %reduce-scatter.15.cloned.1.call-done = bf16[256,256]{1,0:T(8,128)(2,1)} async-done(((bf16[1024,256]{1,0:T(8,128)(2,1)}), bf16[256,256]{1,0:T(8,128)(2,1)}) %reduce-scatter.15.cloned.1.call-update) | async-done | bytes 131088 | tf_op jit(solution)/shard_map/reduce_scatter | solution.py:31
  251.8 1.9 multiply_subtract_fusion.1
  253.7 35.6 %reduce-scatter.17.cloned.1.call-done = bf16[256,256]{1,0:T(8,128)(2,1)} async-done(((bf16[2048,256]{1,0:T(8,128)(2,1)}), bf16[256,256]{1,0:T(8,128)(2,1)}) %reduce-scatter.17.cloned.1.call-update) | async-done | bytes 131088 | tf_op jit(solution)/shard_map/reduce_scatter | solution.py:34
  289.3 1.9 multiply_subtract_fusion
  (39 shorter events, 0.2 us)
Async XLA Ops:
  7.2 29.4 %all-gather.4.cloned.1.call-start = ((), (), s32[]{:S(2)}) async-start(), calls=%async_computation.6 | async-start | bytes 1179648 | tf_op jit(solution)/shard_map/all_gather | solution.py:20
  8.9 72.2 %reduce-scatter.9.cloned.1.call-start = ((), (), s32[]{:S(2)}) async-start(), calls=%async_computation.8 | async-start | bytes 1179648 | tf_op jit(solution)/shard_map/reduce_scatter | solution.py:34
  40.5 2.0 copy-start.3
  42.5 2.5 copy-start.9
  44.9 36.1 %copy-start.1 = (f32[256,256]{1,0:T(8,128)S(1)}, f32[256,256]{1,0:T(8,128)}, u32[]{:S(2)}) copy-start(f32[256,256]{1,0:T(8,128)} %param.13) | copy-start | bytes 786436
  44.9 36.1 %copy-start.6 = (f32[256,256]{1,0:T(8,128)S(1)}, f32[256,256]{1,0:T(8,128)}, u32[]{:S(2)}) copy-start(f32[256,256]{1,0:T(8,128)} %param.15) | copy-start | bytes 786436
  44.9 60.2 %copy-start = (f32[256,256]{1,0:T(8,128)S(1)}, f32[256,256]{1,0:T(8,128)}, u32[]{:S(2)}) copy-start(f32[256,256]{1,0:T(8,128)} %param.12) | copy-start | bytes 786436
  44.9 60.2 %copy-start.5 = (f32[256,256]{1,0:T(8,128)S(1)}, f32[256,256]{1,0:T(8,128)}, u32[]{:S(2)}) copy-start(f32[256,256]{1,0:T(8,128)} %param.14) | copy-start | bytes 786436
  45.0 60.2 %reduce-scatter.7.cloned.1.call-start = ((), (), s32[]{:S(2)}) async-start(), calls=%async_computation.7 | async-start | bytes 655360 | tf_op jit(solution)/shard_map/reduce_scatter | solution.py:31
  49.4 79.8 %all-gather.6.cloned.1.call-start = ((), (), s32[]{:S(2)}) async-start(), calls=%async_computation.9 | async-start | bytes 1179648 | tf_op jit(solution)/shard_map/all_gather | solution.py:20
  82.7 90.9 %reduce-scatter.13.cloned.1.call-start = ((), (), s32[]{:S(2)}) async-start(), calls=%async_computation.11 | async-start | bytes 1179648 | tf_op jit(solution)/shard_map/reduce_scatter | solution.py:34
  133.1 2.0 copy-start.4
  135.0 2.5 copy-start.10
  137.5 36.1 %copy-start.7 = (bf16[256,256]{1,0:T(8,128)(2,1)S(1)}, bf16[256,256]{1,0:T(8,128)(2,1)}, u32[]{:S(2)}) copy-start(bf16[256,256]{1,0:T(8,128)(2,1)} %reduce-scatter.9.cloned.1.call-done) | copy-start | bytes 393220
  137.5 60.1 %copy-start.8 = (bf16[256,256]{1,0:T(8,128)(2,1)S(1)}, bf16[256,256]{1,0:T(8,128)(2,1)}, u32[]{:S(2)}) copy-start(bf16[256,256]{1,0:T(8,128)(2,1)} %reduce-scatter.7.cloned.1.call-done) | copy-start | bytes 393220
  137.5 60.1 %reduce-scatter.11.cloned.1.call-start = ((), (), s32[]{:S(2)}) async-start(), calls=%async_computation.10 | async-start | bytes 655360 | tf_op jit(solution)/shard_map/reduce_scatter | solution.py:31
  141.9 79.9 %all-gather.8.cloned.1.call-start = ((), (), s32[]{:S(2)}) async-start(), calls=%async_computation.12 | async-start | bytes 1179648 | tf_op jit(solution)/shard_map/all_gather | solution.py:20
  175.3 76.5 %reduce-scatter.15.cloned.1.call-start = ((), (), s32[]{:S(2)}) async-start(), calls=%async_computation.13 | async-start | bytes 655360 | tf_op jit(solution)/shard_map/reduce_scatter | solution.py:31
  221.7 6.0 %copy-start.11 = (bf16[2048,256]{1,0:T(8,128)(2,1)S(1)}, bf16[2048,256]{1,0:T(8,128)(2,1)}, u32[]{:S(2)}) copy-start(bf16[2048,256]{1,0:T(8,128)(2,1)} %all-gather.8.cloned.1.call-done) | copy-start | bytes 3145732
  225.8 2.0 copy-start.2
  229.8 4.7 %copy-start.14 = (s32[2]{0:T(128)S(1)}, s32[2]{0:T(128)}, u32[]{:S(2)}) copy-start(s32[2]{0:T(128)} %param.16) | copy-start | bytes 28
  229.8 4.8 %copy-start.15 = (s32[2]{0:T(128)S(1)}, s32[2]{0:T(128)}, u32[]{:S(2)}) copy-start(s32[2]{0:T(128)} %param.17) | copy-start | bytes 28
  229.9 22.0 %copy-start.13 = (bf16[256,256]{1,0:T(8,128)(2,1)S(1)}, bf16[256,256]{1,0:T(8,128)(2,1)}, u32[]{:S(2)}) copy-start(bf16[256,256]{1,0:T(8,128)(2,1)} %reduce-scatter.11.cloned.1.call-done) | copy-start | bytes 393220
  229.9 59.4 %copy-start.12 = (bf16[256,256]{1,0:T(8,128)(2,1)S(1)}, bf16[256,256]{1,0:T(8,128)(2,1)}, u32[]{:S(2)}) copy-start(bf16[256,256]{1,0:T(8,128)(2,1)} %reduce-scatter.13.cloned.1.call-done) | copy-start | bytes 393220
  229.9 59.4 %reduce-scatter.17.cloned.1.call-start = ((), (), s32[]{:S(2)}) async-start(), calls=%async_computation.14 | async-start | bytes 1179648 | tf_op jit(solution)/shard_map/reduce_scatter | solution.py:34
Sparse Core Ops, SparseCore 0:
  10.4 26.0 all-gather.3
  45.0 35.9 reduce-scatter.8
  83.3 21.8 reduce-scatter.6
  107.5 21.5 all-gather.5
  137.6 35.9 reduce-scatter.12
  175.7 21.8 reduce-scatter.10
  200.0 21.6 all-gather.7
  230.0 21.8 reduce-scatter.14
  255.0 34.2 reduce-scatter.16
where the time goes:
time: 298 us
  waiting for transfers between devices  184 us (62%)
  blocking collectives  48.3 us (16%)
  matrix products  32 us (11%)
  between operations  14.7 us (5%)
  other arithmetic  12.3 us (4%)
  local copies, waits for them, and re-layouts  6.19 us (2%)
    reduce_scatter x3, waiting for transfers between devices, gradients(): lax.psum_scatter(item_sum.astype(jnp.bfloat16), 'usr', scatter_dimension=...  98.9 us
    reduce_scatter x3, waiting for transfers between devices, gradients(): lax.psum_scatter(user_sum.astype(jnp.bfloat16), 'itm', scatter_dimension=...  61.8 us
    all_gather x3, blocking collectives, gradients(): lax.all_gather(user_pos.astype(jnp.bfloat16), 'itm', axis=0, tiled=True)  48.3 us
    all_gather x3, waiting for transfers between devices, gradients(): lax.all_gather(item_pos.astype(jnp.bfloat16), 'usr', axis=0, tiled=True)  23 us
    dot_general x3, matrix products, gradients(): guess = jnp.dot(full_users, piece.T, preferred_element_type=jnp.float32)  12 us
    dot_general x3, matrix products, gradients(): user_sum = jnp.dot(error, piece, preferred_element_type=jnp.float32)  10.7 us
    dot_general x3, matrix products, gradients(): item_part = jnp.dot(error.T, full_users, preferred_element_type=jnp.float32)  9.37 us
  transfers between devices with their start and end apart: 9, of which 9 were waited for; matrix products, arithmetic and copies ran while one was open for 7% of the time, Pallas kernels for 0%

commit v1 on v0

v1 whole, which is shorter than its diff:
```python
import functools

import jax
import jax.numpy as jnp
from jax import lax
from jax.experimental import pallas as pl
from jax.experimental.pallas import tpu as pltpu
from jax.sharding import PartitionSpec as P

BLK = 128
LEAPS = 2
STEP = 0.02
GRADS = LEAPS + 1
CHUNK = 512
SUB = 2

BF = jnp.bfloat16
F32 = jnp.float32


def flip(index, toggle, bits):
    out = index
    for b in range(bits):
        if (toggle >> b) & 1:
            out = out + (1 - 2 * ((index // (1 << b)) % 2)) * (1 << b)
    return out


def nearest(z, k, n):
    m = jnp.minimum(z, n - 1 - z)
    half = (k + 1) // 2
    around = z + half * (1 - 2 * (k % 2))
    beyond = jnp.where(z < n - 1 - z, k, n - 1 - k)
    return jnp.where(k <= 2 * m, around, beyond)


def kernel(
    n_usr, n_itm,
    ratings_hbm, colmask, counts, users, items, user_mom, item_mom,
    upos, ipos, umom, imom,
    rate, ufull, vfull, usend, urecv, uown, iacc, ipsend, iprecv, csend, crecv, iown,
    rsem, zs, zr, vs, vr, vf, us, ur, ps, pr, cs, cr,
):
    z = lax.axis_index("itm")
    me = lax.axis_index("usr")
    core = me % 2
    chip = me // 2
    nc = n_usr // 2
    bits = nc.bit_length() - 1
    up, k_dim = users.shape
    ip = items.shape[0]
    n_items = rate.shape[1]
    sub = up // SUB

    def remote(src, dst, ssem, rsem_, usr, itm):
        return pltpu.make_async_remote_copy(
            src_ref=src, dst_ref=dst, send_sem=ssem, recv_sem=rsem_,
            device_id={"usr": usr, "itm": itm}, device_id_type=pl.DeviceIdType.MESH)

    partner = chip * 2 + (1 - core)

    def peer(t):
        return flip(chip, t, bits)

    def z_copy(g, piece, s, direction, to):
        rows = pl.ds(pl.multiple_of(piece * up + s * sub, sub), sub)
        return remote(ufull.at[g, rows], ufull.at[g, rows], zs.at[g, direction, piece, s], zr.at[g, piece, s], me, to)

    def v_rows(piece):
        return pl.ds(pl.multiple_of(piece * ip, ip), ip)

    def v_peer(g, q):
        return remote(vfull.at[g, v_rows(me)], vfull.at[g, v_rows(me)], vs.at[g, q], vr.at[g, me], q * 2 + core, z)

    def v_partner(g, q):
        piece = q * 2 + core
        return remote(vfull.at[g, v_rows(piece)], vfull.at[g, v_rows(piece)], vf.at[g, q], vr.at[g, piece], partner, z)

    def v_arrival(g, piece):
        return remote(vfull.at[g, v_rows(piece)], vfull.at[g, v_rows(piece)], vf.at[g, 0], vr.at[g, piece], partner, z)

    def u_part(g, to):
        return remote(usend.at[g, to], urecv.at[g, z], us.at[g, to], ur.at[g, z], me, to)

    def u_arrival(g, origin):
        return remote(usend.at[g, 0], urecv.at[g, origin], us.at[g, 0], ur.at[g, origin], me, origin)

    def p_part(g, q):
        return remote(ipsend.at[g, q], iprecv.at[g, q], ps.at[g, q], pr.at[g, q], partner, z)

    def c_part(g, q):
        return remote(csend.at[g, q], crecv.at[g, chip], cs.at[g, q], cr.at[g, chip], q * 2 + core, z)

    def c_arrival(g, q):
        return remote(csend.at[g, q], crecv.at[g, q], cs.at[g, q], cr.at[g, q], q * 2 + core, z)

    def send_users(g):
        ufull[g, pl.ds(pl.multiple_of(z * up, up), up), :] = upos[...].astype(BF)
        for s in range(SUB):
            @pl.when(z + 1 < n_itm)
            def _():
                z_copy(g, z, s, 0, z + 1).start()

            @pl.when(z > 0)
            def _():
                z_copy(g, z, s, 1, z - 1).start()

    def send_items(g):
        vfull[g, v_rows(me), :] = ipos[...].astype(BF)
        for t in range(1, nc):
            v_peer(g, peer(t)).start()
        v_partner(g, chip).start()

    load = pltpu.make_async_copy(ratings_hbm, rate, rsem)
    load.start()

    upos[...] = users[...]
    ipos[...] = items[...]
    umom[...] = user_mom[...]
    imom[...] = item_mom[...]

    barrier = pltpu.get_barrier_semaphore()
    for d in range(1, n_itm):
        pl.semaphore_signal(barrier, inc=1, device_id={"usr": me, "itm": (z + d) % n_itm}, device_id_type=pl.DeviceIdType.MESH)
    for t in range(1, nc):
        pl.semaphore_signal(barrier, inc=1, device_id={"usr": peer(t) * 2 + core, "itm": z}, device_id_type=pl.DeviceIdType.MESH)
    pl.semaphore_signal(barrier, inc=1, device_id={"usr": partner, "itm": z}, device_id_type=pl.DeviceIdType.MESH)
    pl.semaphore_wait(barrier, n_itm - 1 + nc - 1 + 1)

    send_users(0)
    send_items(0)
    load.wait()

    def z_step(g, k):
        piece = nearest(z, k, n_itm)
        for s in range(SUB):
            z_copy(g, piece, s, 0, piece).wait_recv()

            @pl.when((piece < z) & (z + 1 < n_itm))
            def _():
                z_copy(g, piece, s, 0, z + 1).start()

            @pl.when((piece > z) & (z > 0))
            def _():
                z_copy(g, piece, s, 1, z - 1).start()

    def v_step(g, t):
        q = peer(t)
        v_arrival(g, q * 2 + core).wait_recv()
        v_partner(g, q).start()

    def gradient(g, carry):
        for t in range(1, max(nc, n_itm)):
            if t < n_itm:
                z_step(g, t)
            if t < nc:
                v_step(g, t)
        for t in range(nc):
            v_arrival(g, peer(t) * 2 + (1 - core)).wait_recv()

        def user_piece(k, carry):
            piece = nearest(z, n_itm - 1 - k, n_itm)
            rows = pl.ds(pl.multiple_of(piece * up, up), up)
            u = ufull[g, rows, :]
            alive = [
                ((piece * up + b * BLK + lax.broadcasted_iota(jnp.int32, (BLK, 1), 0)) < counts[0]).astype(F32)
                for b in range(up // BLK)
            ]
            usum = jnp.zeros((up, k_dim), F32)
            for c0 in range(0, n_items, CHUNK):
                v = vfull[g, c0:c0 + CHUNK, :]
                guess = lax.dot_general(u, v, (((1,), (1,)), ((), ())), preferred_element_type=F32)
                diff = rate[rows, c0:c0 + CHUNK].astype(F32) - guess
                parts = []
                for b in range(up // BLK):
                    live = colmask[pl.ds(piece * (up // BLK) + b, 1), c0:c0 + CHUNK]
                    parts.append((diff[b * BLK:(b + 1) * BLK] * live * alive[b]).astype(BF))
                err = jnp.concatenate(parts, axis=0) if len(parts) > 1 else parts[0]
                usum = usum + jnp.dot(err, v, preferred_element_type=F32)
                iacc[c0:c0 + CHUNK, :] += lax.dot_general(err, u, (((0,), (0,)), ((), ())), preferred_element_type=F32)

            @pl.when(piece == z)
            def _():
                uown[...] = usum

            @pl.when(piece != z)
            def _():
                usend[g, piece] = usum.astype(BF)
                u_part(g, piece).start()
            return carry

        iacc[...] = jnp.zeros_like(iacc)
        lax.fori_loop(0, n_itm, user_piece, 0)

        for t in range(nc - 1, -1, -1):
            q = peer(t)
            ipsend[g, q] = iacc[v_rows(q * 2 + 1 - core), :].astype(BF)
            p_part(g, q).start()
        for t in range(nc - 1, -1, -1):
            q = peer(t)
            p_part(g, q).wait_recv()
            both = iacc[v_rows(q * 2 + core), :] + iprecv[g, q].astype(F32)
            if t:
                csend[g, q] = both.astype(BF)
                c_part(g, q).start()
            else:
                iown[...] = both

        scale = jnp.where((g == 0) | (g == GRADS - 1), 0.5 * STEP, STEP)
        total = uown[...]
        for d in range(1, n_itm):
            origin = (z + d) % n_itm
            u_arrival(g, origin).wait_recv()
            total = total + urecv[g, origin].astype(F32)
        umom[...] = umom[...] - scale * (upos[...] - total)

        @pl.when(g < GRADS - 1)
        def _():
            upos[...] = upos[...] + STEP * umom[...]
            send_users(g + 1)

        total = iown[...]
        for t in range(1, nc):
            q = peer(t)
            c_arrival(g, q).wait_recv()
            total = total + crecv[g, q].astype(F32)
        imom[...] = imom[...] - scale * (ipos[...] - total)

        @pl.when(g < GRADS - 1)
        def _():
            ipos[...] = ipos[...] + STEP * imom[...]
            send_items(g + 1)

        def sent(piece, carry):
            for s in range(SUB):
                @pl.when((piece <= z) & (z + 1 < n_itm))
                def _():
                    z_copy(g, piece, s, 0, z + 1).wait_send()

                @pl.when((piece >= z) & (z > 0))
                def _():
                    z_copy(g, piece, s, 1, z - 1).wait_send()

            @pl.when(piece != z)
            def _():
                u_part(g, piece).wait_send()
            return carry

        lax.fori_loop(0, n_itm, sent, 0)
        for t in range(nc):
            q = peer(t)
            v_partner(g, q).wait_send()
            p_part(g, q).wait_send()
            if t:
                v_peer(g, q).wait_send()
                c_part(g, q).wait_send()
        return carry

    lax.fori_loop(0, GRADS, gradient, 0)


def body(n_usr, n_itm, ratings, tile_mask, counts, users, items, user_mom, item_mom, user_accept, item_accept):
    colmask = jnp.repeat(tile_mask, BLK, axis=1).astype(F32)
    up, k_dim = users.shape
    ip = items.shape[0]
    nc = n_usr // 2
    dma = pltpu.SemaphoreType.DMA
    vmem = pl.BlockSpec(memory_space=pltpu.VMEM)
    G = GRADS
    user_pos, item_pos, user_mom, item_mom = pl.pallas_call(
        functools.partial(kernel, n_usr, n_itm),
        out_shape=[jax.ShapeDtypeStruct((up, k_dim), F32), jax.ShapeDtypeStruct((ip, k_dim), F32)] * 2,
        in_specs=[pl.BlockSpec(memory_space=pl.ANY), vmem, pl.BlockSpec(memory_space=pltpu.SMEM), vmem, vmem, vmem, vmem],
        out_specs=[vmem] * 4,
        scratch_shapes=[
            pltpu.VMEM(ratings.shape, BF),
            pltpu.VMEM((G, up * n_itm, k_dim), BF),
            pltpu.VMEM((G, ip * n_usr, k_dim), BF),
            pltpu.VMEM((G, n_itm, up, k_dim), BF),
            pltpu.VMEM((G, n_itm, up, k_dim), BF),
            pltpu.VMEM((up, k_dim), F32),
            pltpu.VMEM((ip * n_usr, k_dim), F32),
            pltpu.VMEM((G, nc, ip, k_dim), BF),
            pltpu.VMEM((G, nc, ip, k_dim), BF),
            pltpu.VMEM((G, nc, ip, k_dim), BF),
            pltpu.VMEM((G, nc, ip, k_dim), BF),
            pltpu.VMEM((ip, k_dim), F32),
            dma,
            dma((G, 2, n_itm, SUB)), dma((G, n_itm, SUB)),
            dma((G, nc)), dma((G, n_usr)), dma((G, nc)),
            dma((G, n_itm)), dma((G, n_itm)),
            dma((G, nc)), dma((G, nc)),
            dma((G, nc)), dma((G, nc)),
        ],
        compiler_params=pltpu.CompilerParams(
            collective_id=0, has_side_effects=True, vmem_limit_bytes=56 * 1024 * 1024),
    )(ratings, colmask, counts, users, items, user_mom, item_mom)
    user_take = jnp.repeat(user_accept, BLK)[:, None] > 0
    item_take = jnp.repeat(item_accept, BLK)[:, None] > 0
    return (
        jnp.where(user_take, user_pos, users),
        jnp.where(item_take, item_pos, items),
        user_mom,
        item_mom,
    )


def solution(mesh):
    in_specs = (
        P("usr", "itm"),
        P("usr", "itm"),
        P("usr"),
        P(("usr", "itm"), None),
        P(("itm", "usr"), None),
        P(("usr", "itm"), None),
        P(("itm", "usr"), None),
        P(("usr", "itm")),
        P(("itm", "usr")),
    )
    out_specs = (
        P(("usr", "itm"), None),
        P(("itm", "usr"), None),
        P(("usr", "itm"), None),
        P(("itm", "usr"), None),
    )
    return jax.shard_map(
        functools.partial(body, mesh.shape["usr"], mesh.shape["itm"]),
        mesh=mesh, in_specs=in_specs, out_specs=out_specs, check_vma=False)
```

time: 298 us -> 106 us (0.36)
  waiting for transfers between devices: 184 us -> 0 us
  Pallas kernels: 0 us -> 96.1 us
  blocking collectives: 48.3 us -> 0 us
  matrix products: 32 us -> 0 us
  between operations: 14.7 us -> 1.38 us
  other arithmetic: 12.3 us -> 3.97 us
    reduce_scatter x6 -> x0, waiting for transfers between devices: 161 us -> none  [the longest x3 98.9 us: gradients(): lax.psum_scatter(item_sum.astype(jnp.bfloat16), 'usr', scatter_dimension=...]
    pallas_call x0 -> x1, Pallas kernels: none -> 96.1 us  [body(): pl.pallas_call(functools.partial(kernel, n_usr, n_itm), out_shape=[jax.Sh...]
    all_gather x3 -> x0, blocking collectives: 48.3 us -> none  [gradients(): lax.all_gather(user_pos.astype(jnp.bfloat16), 'itm', axis=0, tiled=True)]
    dot_general x9 -> x0, matrix products: 32 us -> none  [the longest x3 12 us: gradients(): guess = jnp.dot(full_users, piece.T, preferred_element_type=jnp.float32)]
    all_gather x3 -> x0, waiting for transfers between devices: 23 us -> none  [gradients(): lax.all_gather(item_pos.astype(jnp.bfloat16), 'usr', axis=0, tiled=True)]
    convert_element_type x8 -> x1, other arithmetic: 8.57 us -> 0.69 us  [body(): colmask = jnp.repeat(tile_mask, BLK, axis=1).astype(F32)]
    sub x2 -> x0, other arithmetic: 3.71 us -> none  [the longest x1 1.86 us: body(): user_mom = user_mom - 0.5 * step_size * user_grad]
  transfers between devices with their start and end apart: 9 -> 0, of which waited for: 9 -> 0; matrix products, arithmetic and copies ran while one was open for 7% -> 0% of each run, Pallas kernels for 0% -> 0%
where the time goes in v1:
time: 106 us
  Pallas kernels  96.1 us (91%)
  local copies, waits for them, and re-layouts  4.29 us (4%)
  other arithmetic  3.97 us (4%)
  between operations  1.38 us (1%)
    pallas_call x1, Pallas kernels, body(): pl.pallas_call(functools.partial(kernel, n_usr, n_itm), out_shape=[jax.Sh...  96.1 us
    unnamed x6, local copies, waits for them, and re-layouts  3.35 us

profile of v1, /device:TPU:0, one launch (start us, length us, event | category | flops | bytes accessed | tf_op | source)
XLA Modules:
  0.0 105.7 jit_solution(713555917906367035)
XLA Ops:
  0.6 0.0 copy-start.1
  0.6 0.0 copy-start
  1.4 0.7 broadcast_compare_fusion.1
  2.0 0.1 broadcast_bitcast_fusion.2
  2.1 0.7 broadcast_compare_fusion
  2.8 0.1 broadcast_bitcast_fusion.1
  2.8 0.7 convert_element_type.5
  3.5 0.1 copy.13
  3.6 0.7 broadcast_bitcast_fusion.colmask
  4.3 96.1 %shard_map.120 = (f32[256,256]{1,0:T(8,128)}, f32[256,256]{1,0:T(8,128)}, f32[256,256]{1,0:T(8,128)}, f32[256,256]{1,0:T(8,128)}) custom-call(bf16[1024,2048]{1,0:T(8,128)(2,1)} %ratings_hbm.1, f32[8,2048]{1,0:T(8,128)} %broadcast_bitcast_fusion.colmask, s32[1]{0:T(128)S(6)} %copy.16.counts, f32[256,256]{1,0:T(8,128)} %users.1, f32[256,256]{1,0:T(8,128)} %items.1, ...), custom_call_target="tpu_custom_call" | custom-call | tf_op jit(solution)/shard_map/pallas_call | solution.py:270
  100.4 0.0 copy-done.1
  100.4 0.0 copy-done
  100.4 2.0 %broadcast_select_fusion = (f32[256,256]{1,0:T(8,128)}, f32[256,256]{1,0:T(8,128)}) fusion(f32[256,256]{1,0:T(8,128)} %get-tuple-element.9, f32[256,256]{1,0:T(8,128)S(1)} %copy-done.1, pred[256]{0:T(512)(128)(4,1)S(1)} %broadcast_bitcast_fusion.1, f32[256,256]{1,0:T(8,128)} %get-tuple-element.8, f32[256,256]{1,0:T(8,128)S(1)} %copy-done, ...), kind=kLoop, calls=%fused_computation | loop fusion | flops 131072 | bytes 1573376 | tf_op jit(solution)/shard_map/jit(_where)/select_n | solution.py:302
  102.4 1.7 %copy.17 = f32[256,256]{1,0:T(8,128)} copy(f32[256,256]{1,0:T(8,128)} %get-tuple-element.20) | data formatting | bytes 524288
  104.0 1.7 %copy.18 = f32[256,256]{1,0:T(8,128)} copy(f32[256,256]{1,0:T(8,128)} %get-tuple-element.21) | data formatting | bytes 524288
Async XLA Ops:
  0.6 99.8 %copy-start.1 = (f32[256,256]{1,0:T(8,128)S(1)}, f32[256,256]{1,0:T(8,128)}, u32[]{:S(2)}) copy-start(f32[256,256]{1,0:T(8,128)} %items.1) | copy-start | bytes 786436
  0.6 99.8 %copy-start = (f32[256,256]{1,0:T(8,128)S(1)}, f32[256,256]{1,0:T(8,128)}, u32[]{:S(2)}) copy-start(f32[256,256]{1,0:T(8,128)} %users.1) | copy-start | bytes 786436

commit v2 on v1

--- a/solution.py
+++ b/solution.py
@@ -11,7 +11,6 @@
 LEAPS = 2
 STEP = 0.02
 GRADS = LEAPS + 1
-CHUNK = 512
 SUB = 2
 
 BF = jnp.bfloat16
@@ -36,9 +35,9 @@
 
 def kernel(
     n_usr, n_itm,
-    ratings_hbm, colmask, counts, users, items, user_mom, item_mom,
-    upos, ipos, umom, imom,
-    rate, ufull, vfull, usend, urecv, uown, iacc, ipsend, iprecv, csend, crecv, iown,
+    ratings_hbm, tile_mask, counts, users, items, user_mom, item_mom,
+    upos, ipos, umom, imom, utot, itot,
+    rate, colmask, ufull, vfull, usend, urecv, uown, iacc, ipsend, iprecv, csend, crecv, iown,
     rsem, zs, zr, vs, vr, vf, us, ur, ps, pr, cs, cr,
 ):
     z = lax.axis_index("itm")
@@ -83,7 +82,7 @@
         return remote(usend.at[g, to], urecv.at[g, z], us.at[g, to], ur.at[g, z], me, to)
 
     def u_arrival(g, origin):
-        return remote(usend.at[g, 0], urecv.at[g, origin], us.at[g, 0], ur.at[g, origin], me, origin)
+        return remote(usend.at[g, origin], urecv.at[g, origin], us.at[g, origin], ur.at[g, origin], me, origin)
 
     def p_part(g, q):
         return remote(ipsend.at[g, q], iprecv.at[g, q], ps.at[g, q], pr.at[g, q], partner, z)
@@ -118,6 +117,10 @@
     ipos[...] = items[...]
     umom[...] = user_mom[...]
     imom[...] = item_mom[...]
+
+    for r in range(colmask.shape[0]):
+        for c in range(colmask.shape[1] // BLK):
+            colmask[r:r + 1, c * BLK:(c + 1) * BLK] = jnp.full((1, BLK), tile_mask[r, c], jnp.int32).astype(F32)
 
     barrier = pltpu.get_barrier_semaphore()
     for d in range(1, n_itm):
@@ -151,15 +154,14 @@
 
     def gradient(g, carry):
         for t in range(1, max(nc, n_itm)):
+            if t < nc:
+                v_step(g, t)
             if t < n_itm:
                 z_step(g, t)
-            if t < nc:
-                v_step(g, t)
         for t in range(nc):
             v_arrival(g, peer(t) * 2 + (1 - core)).wait_recv()
 
-        def user_piece(k, carry):
-            piece = nearest(z, n_itm - 1 - k, n_itm)
+        def terms(piece, chunk, after):
             rows = pl.ds(pl.multiple_of(piece * up, up), up)
             u = ufull[g, rows, :]
             alive = [
@@ -167,55 +169,68 @@
                 for b in range(up // BLK)
             ]
             usum = jnp.zeros((up, k_dim), F32)
-            for c0 in range(0, n_items, CHUNK):
-                v = vfull[g, c0:c0 + CHUNK, :]
+            for c0 in range(0, n_items, chunk):
+                v = vfull[g, c0:c0 + chunk, :]
                 guess = lax.dot_general(u, v, (((1,), (1,)), ((), ())), preferred_element_type=F32)
-                diff = rate[rows, c0:c0 + CHUNK].astype(F32) - guess
+                diff = rate[rows, c0:c0 + chunk].astype(F32) - guess
                 parts = []
                 for b in range(up // BLK):
-                    live = colmask[pl.ds(piece * (up // BLK) + b, 1), c0:c0 + CHUNK]
+                    live = colmask[pl.ds(piece * (up // BLK) + b, 1), c0:c0 + chunk]
                     parts.append((diff[b * BLK:(b + 1) * BLK] * live * alive[b]).astype(BF))
                 err = jnp.concatenate(parts, axis=0) if len(parts) > 1 else parts[0]
                 usum = usum + jnp.dot(err, v, preferred_element_type=F32)
-                iacc[c0:c0 + CHUNK, :] += lax.dot_general(err, u, (((0,), (0,)), ((), ())), preferred_element_type=F32)
-
-            @pl.when(piece == z)
-            def _():
-                uown[...] = usum
-
-            @pl.when(piece != z)
-            def _():
-                usend[g, piece] = usum.astype(BF)
-                u_part(g, piece).start()
+                iacc[c0:c0 + chunk, :] += lax.dot_general(err, u, (((0,), (0,)), ((), ())), preferred_element_type=F32)
+                if after is not None:
+                    after(c0 // chunk)
+            return usum
+
+        def user_piece(k, carry):
+            piece = nearest(z, n_itm - 1 - k, n_itm)
+            usum = terms(piece, n_items, None)
+
+            usend[g, piece] = usum.astype(BF)
+            u_part(g, piece).start()
             return carry
 
-        iacc[...] = jnp.zeros_like(iacc)
-        lax.fori_loop(0, n_itm, user_piece, 0)
-
-        for t in range(nc - 1, -1, -1):
-            q = peer(t)
+        def hand_over(q):
             ipsend[g, q] = iacc[v_rows(q * 2 + 1 - core), :].astype(BF)
             p_part(g, q).start()
-        for t in range(nc - 1, -1, -1):
-            q = peer(t)
+
+        def both_cores(q):
             p_part(g, q).wait_recv()
             both = iacc[v_rows(q * 2 + core), :] + iprecv[g, q].astype(F32)
-            if t:
+
+            @pl.when(q == chip)
+            def _():
+                iown[...] = both
+
+            @pl.when(q != chip)
+            def _():
                 csend[g, q] = both.astype(BF)
                 c_part(g, q).start()
-            else:
-                iown[...] = both
-
-        scale = jnp.where((g == 0) | (g == GRADS - 1), 0.5 * STEP, STEP)
+
+        def after(q):
+            hand_over(q)
+            if q >= 2:
+                both_cores(q - 2)
+
+        iacc[...] = jnp.zeros_like(iacc)
+        lax.fori_loop(0, n_itm - 1, user_piece, 0)
+        uown[...] = terms(z, n_items // nc, after)
+        for q in range(max(nc - 2, 0), nc):
+            both_cores(q)
+
+        scale = jnp.where(g == 0, 0.5 * STEP, STEP)
         total = uown[...]
         for d in range(1, n_itm):
             origin = (z + d) % n_itm
             u_arrival(g, origin).wait_recv()
             total = total + urecv[g, origin].astype(F32)
-        umom[...] = umom[...] - scale * (upos[...] - total)
+        utot[...] = total
 
         @pl.when(g < GRADS - 1)
         def _():
+            umom[...] = umom[...] - scale * (upos[...] - utot[...])
             upos[...] = upos[...] + STEP * umom[...]
             send_users(g + 1)
 
@@ -224,10 +239,11 @@
             q = peer(t)
             c_arrival(g, q).wait_recv()
             total = total + crecv[g, q].astype(F32)
-        imom[...] = imom[...] - scale * (ipos[...] - total)
+        itot[...] = total
 
         @pl.when(g < GRADS - 1)
         def _():
+            imom[...] = imom[...] - scale * (ipos[...] - itot[...])
             ipos[...] = ipos[...] + STEP * imom[...]
             send_items(g + 1)
 
@@ -260,20 +276,20 @@
 
 
 def body(n_usr, n_itm, ratings, tile_mask, counts, users, items, user_mom, item_mom, user_accept, item_accept):
-    colmask = jnp.repeat(tile_mask, BLK, axis=1).astype(F32)
     up, k_dim = users.shape
     ip = items.shape[0]
     nc = n_usr // 2
     dma = pltpu.SemaphoreType.DMA
     vmem = pl.BlockSpec(memory_space=pltpu.VMEM)
     G = GRADS
-    user_pos, item_pos, user_mom, item_mom = pl.pallas_call(
+    upos, ipos, umom, imom, utot, itot = pl.pallas_call(
         functools.partial(kernel, n_usr, n_itm),
-        out_shape=[jax.ShapeDtypeStruct((up, k_dim), F32), jax.ShapeDtypeStruct((ip, k_dim), F32)] * 2,
-        in_specs=[pl.BlockSpec(memory_space=pl.ANY), vmem, pl.BlockSpec(memory_space=pltpu.SMEM), vmem, vmem, vmem, vmem],
-        out_specs=[vmem] * 4,
+        out_shape=[jax.ShapeDtypeStruct((up, k_dim), F32), jax.ShapeDtypeStruct((ip, k_dim), F32)] * 3,
+        in_specs=[pl.BlockSpec(memory_space=pl.ANY), pl.BlockSpec(memory_space=pltpu.SMEM), pl.BlockSpec(memory_space=pltpu.SMEM), vmem, vmem, vmem, vmem],
+        out_specs=[vmem] * 6,
         scratch_shapes=[
             pltpu.VMEM(ratings.shape, BF),
+            pltpu.VMEM((ratings.shape[0] // BLK, ratings.shape[1]), F32),
             pltpu.VMEM((G, up * n_itm, k_dim), BF),
             pltpu.VMEM((G, ip * n_usr, k_dim), BF),
             pltpu.VMEM((G, n_itm, up, k_dim), BF),
@@ -293,15 +309,15 @@
             dma((G, nc)), dma((G, nc)),
         ],
         compiler_params=pltpu.CompilerParams(
-            collective_id=0, has_side_effects=True, vmem_limit_bytes=56 * 1024 * 1024),
-    )(ratings, colmask, counts, users, items, user_mom, item_mom)
+            collective_id=0, has_side_effects=True, vmem_limit_bytes=40 * 1024 * 1024),
+    )(ratings, tile_mask, counts, users, items, user_mom, item_mom)
     user_take = jnp.repeat(user_accept, BLK)[:, None] > 0
     item_take = jnp.repeat(item_accept, BLK)[:, None] > 0
     return (
-        jnp.where(user_take, user_pos, users),
-        jnp.where(item_take, item_pos, items),
-        user_mom,
-        item_mom,
+        jnp.where(user_take, upos, users),
+        jnp.where(item_take, ipos, items),
+        umom - 0.5 * STEP * (upos - utot),
+        imom - 0.5 * STEP * (ipos - itot),
     )
 
 

time: 106 us -> 102 us (0.962)
  Pallas kernels: 96.1 us -> 90.8 us
  local copies, waits for them, and re-layouts: 4.29 us -> 6.82 us
  other arithmetic: 3.97 us -> 2.39 us
    pallas_call x1, Pallas kernels: 96.1 us -> 90.8 us  [body(): pl.pallas_call(functools.partial(kernel, n_usr, n_itm), out_shape=[jax.Sh...]
    unnamed x6 -> x12, local copies, waits for them, and re-layouts: 3.35 us -> 6.67 us
    select_n x1 -> x0, other arithmetic: 1.96 us -> none  [body(): jnp.where(item_take, item_pos, items)]
    sub x0 -> x1, other arithmetic: none -> 1.07 us  [body(): imom - 0.5 * STEP * (ipos - itot)]
where the time goes in v2:
time: 102 us; the launch traced here: 101 us
  Pallas kernels  90.8 us (89%)
  local copies, waits for them, and re-layouts  6.82 us (7%)
  other arithmetic  2.39 us (2%)
  between operations  1.29 us (1%)
    pallas_call x1, Pallas kernels, body(): pl.pallas_call(functools.partial(kernel, n_usr, n_itm), out_shape=[jax.Sh...  90.8 us
    unnamed x12, local copies, waits for them, and re-layouts  6.67 us

profile of v2, /device:TPU:0, one launch (start us, length us, event | category | flops | bytes accessed | tf_op | source)
XLA Modules:
  0.0 101.3 jit_solution(16551394283083733722)
XLA Ops:
  1.3 0.7 broadcast_compare_fusion.1
  1.9 0.1 broadcast_bitcast_fusion.1
  2.0 0.7 broadcast_compare_fusion
  2.7 0.1 broadcast_bitcast_fusion
  2.7 0.0 copy-start
  2.8 2.2 %copy-done = bf16[1024,2048]{1,0:T(8,128)(2,1)S(1)} copy-done((bf16[1024,2048]{1,0:T(8,128)(2,1)S(1)}, bf16[1024,2048]{1,0:T(8,128)(2,1)}, u32[]{:S(2)}) %copy-start) | copy-done | bytes 4194328
  4.9 0.0 copy-start.1
  4.9 0.9 copy-done.1
  5.9 0.0 copy-start.2
  5.9 0.9 copy-done.2
  6.8 0.0 copy-start.3
  6.8 0.9 copy-done.3
  7.8 0.0 copy-start.4
  7.8 0.9 copy-done.4
  8.7 0.0 copy-start.5
  8.7 0.7 copy-done.5
  9.4 90.8 %shard_map.120 = (f32[256,256]{1,0:T(8,128)S(1)}, f32[256,256]{1,0:T(8,128)S(1)}, f32[256,256]{1,0:T(8,128)S(1)}, f32[256,256]{1,0:T(8,128)S(1)}, f32[256,256]{1,0:T(8,128)S(1)}, /*index=5*/f32[256,256]{1,0:T(8,128)S(1)}) custom-call(bf16[1024,2048]{1,0:T(8,128)(2,1)S(1)} %copy-done, s32[8,16]{1,0:T(8,128)S(1)} %copy-done.5, s32[1]{0:T(128)S(6)} %copy.13.counts, ...), custom_call_target="tpu_custom_call" | custom-call | tf_op jit(solution)/shard_map/pallas_call | solution.py:285
  100.2 1.1 %multiply_subtract_fusion = (f32[256,256]{1,0:T(8,128)}, f32[256,256]{1,0:T(8,128)}, f32[256,256]{1,0:T(8,128)}, f32[256,256]{1,0:T(8,128)}) fusion(f32[256,256]{1,0:T(8,128)S(1)} %get-tuple-element.14, f32[256,256]{1,0:T(8,128)S(1)} %get-tuple-element.11, f32[256,256]{1,0:T(8,128)S(1)} %get-tuple-element.15, f32[256,256]{1,0:T(8,128)S(1)} %copy-done.2, ...), kind=kLoop, calls=%fused_computation | loop fusion | flops 524288 | bytes 3146240 | tf_op jit(solution)/shard_map/sub | solution.py:320
Async XLA Ops:
  2.7 2.2 %copy-start = (bf16[1024,2048]{1,0:T(8,128)(2,1)S(1)}, bf16[1024,2048]{1,0:T(8,128)(2,1)}, u32[]{:S(2)}) copy-start(bf16[1024,2048]{1,0:T(8,128)(2,1)} %ratings_hbm.1) | copy-start | bytes 12582916
  4.9 0.9 copy-start.1
  5.9 0.9 copy-start.2
  6.8 0.9 copy-start.3
  7.8 0.9 copy-start.4
  8.7 0.7 copy-start.5
